TPU v7x, 768 devices: a whole 4x8x12 slice. The times are simulated.
768 devices in a mesh: head: 2 (over core), seq: 48 (over y_hi, z), mp: 8 (over x, y_lo).
Axes of the slice: x: 4, y: 8 (y_hi: 4, y_lo: 2; y = y_hi * 2 + y_lo), z: 12, core: 2. Of those that a mesh axis runs over, the one named last changes fastest.
Arguments:
- trunk: bfloat16 [768, 8192], P('seq', 'mp'), may hold values from -6 to 6
- branch: bfloat16 [2, 768, 8192], P('head', 'seq', 'mp'), may hold values from -6 to 6
- unembed: bfloat16 [18432, 8192], P('seq', 'mp'), may hold values from -0.09375 to 0.09375
- targets: int32 [2, 768], P('head'), may hold values from 0 to 18431
- loss_grad: float32 [2, 768], P('head'), may hold values from 0.25 to 4
Outputs:
- d_branch: bfloat16 [2, 768, 8192], P('head', 'seq', 'mp')
- d_trunk: bfloat16 [768, 8192], P('seq', 'mp')
- d_unembed: float32 [18432, 8192], P('seq', 'mp')
All inputs are finite; a program needn't handle non-finite values.
Results may differ from a plain program's by a relative error of at most 0.0051.
Values may be sent and summed in bfloat16 or wider, within the bound.
A program may use at most 32 MiB of HBM per device.

v0:
```python
import jax
import jax.numpy as jnp
from jax import lax
from jax.sharding import Mesh
from jax.sharding import PartitionSpec as P

SEQ = ("seq_0", "seq_1")
MP = ("mp_0", "mp_1")
SEQ_MP = ("seq_0", "seq_1", "mp_0", "mp_1")


soft_cap = 30.0


def in_blocks(value, dim, devices):
    shape = value.shape
    blocks = value.reshape(*shape[:dim], devices, shape[dim] // devices, *shape[dim + 1 :])
    return jnp.moveaxis(blocks, dim, 0)


def sum_at_owner(value, axis, dim):
    devices = lax.axis_size(axis)
    blocks = lax.all_to_all(in_blocks(value, dim, devices), axis, 0, 0, tiled=True)
    return jnp.sum(blocks, axis=0)


def one_axis_at_a_time(value, axes):
    for axis in axes:
        value = lax.psum(value, axis)
    return value


def sent_to_all(value, axis):
    copies = jnp.broadcast_to(value, (lax.axis_size(axis), *value.shape))
    return lax.all_to_all(copies, axis, split_axis=0, concat_axis=0, tiled=True)


def in_order(blocks, dim):
    shape = list(blocks.shape[1:])
    shape[dim] *= blocks.shape[0]
    return jnp.moveaxis(blocks, 0, dim).reshape(shape)


def collect(value, axis, dim):
    blocks = sent_to_all(value, axis)
    return in_order(blocks, dim)


def own_block(blocks, axes, sequence):
    inside = blocks.shape[1:]
    blocks = blocks.reshape(*(lax.axis_size(a) for a in axes), *inside)
    blocks = jnp.moveaxis(blocks, sequence, range(len(axes))).reshape(-1, *inside)
    for k in sequence:
        blocks = lax.psum_scatter(blocks, axes[k], scatter_dimension=0, tiled=True)
    return blocks[0]


def summed_rows(value, axes, sequence, dim):
    devices = lax.axis_size(axes)
    return own_block(in_blocks(value, dim, devices), axes, sequence)


def taken_together(value, axis):
    return sent_to_all(value, axis).sum(axis=0)


def together(arrays, axis):
    line, at, done = (jnp.concatenate([a.reshape(-1) for a in arrays]), 0, [])
    subtotal = taken_together(line, axis)
    for a in arrays:
        done.append(subtotal[at : at + a.size].reshape(a.shape))
        at += a.size
    return tuple(done)


def shards(trunk, branch, unembed, targets, loss_grad):
    block_rows = unembed.shape[0]
    hidden = (trunk.astype(jnp.float32) + branch[0].astype(jnp.float32)).astype(jnp.bfloat16)
    gathered = lax.all_gather(hidden, SEQ, axis=0, tiled=True)
    seq_index = lax.axis_index(SEQ)
    share_rows = block_rows // lax.axis_size(MP)
    scores = sum_at_owner(
        lax.dot_general(
            unembed, gathered, (((1,), (1,)), ((), ())), preferred_element_type=jnp.float32
        ),
        MP,
        0,
    )
    first_vocab = seq_index * block_rows + lax.axis_index(MP) * share_rows
    squashed = jnp.tanh(scores / soft_cap)
    exponent = jnp.exp(soft_cap * squashed)
    totals = one_axis_at_a_time(jnp.sum(exponent, axis=0), SEQ_MP)
    vocab_ids = first_vocab + lax.iota(jnp.int32, scores.shape[0])
    onehot = (vocab_ids[:, None] == targets[0][None, :]).astype(jnp.float32)
    slope = (
        loss_grad[0][None, :] * (exponent / totals[None, :] - onehot) * (1.0 - squashed * squashed)
    )
    grad_logits = slope.astype(jnp.bfloat16)
    grad_logits = collect(grad_logits, MP, 0)
    weight_grad = jnp.dot(grad_logits, gathered, preferred_element_type=jnp.float32)
    row_grad = summed_rows(
        lax.dot_general(
            grad_logits, unembed, (((0,), (0,)), ((), ())), preferred_element_type=jnp.float32
        ),
        SEQ,
        (1, 0),
        0,
    )
    trunk_sum, unembed_sum = together((row_grad, weight_grad), "head")
    return (row_grad.astype(jnp.bfloat16)[None], trunk_sum.astype(jnp.bfloat16), unembed_sum)


def solution(mesh):
    split = Mesh(
        mesh.devices.reshape(mesh.shape["head"], 4, 12, 4, 2),
        ("head", "seq_0", "seq_1", "mp_0", "mp_1"),
    )
    return jax.shard_map(
        shards,
        mesh=split,
        in_specs=(P(SEQ, MP), P("head", SEQ, MP), P(SEQ, MP), P("head", None), P("head", None)),
        out_specs=(P("head", SEQ, MP), P(SEQ, MP), P(SEQ, MP)),
        check_vma=False,
    )
```

profile of v0, /device:TPU:1, one launch (start us, length us, event | category | flops | bytes accessed | tf_op | source)
XLA Modules:
  0.0 355.2 jit_solution(7854131368290880563)
XLA Ops:
  7.2 0.0 copy-start
  7.2 0.0 all-gather.2.cloned.1.call-start
  7.2 1.5 fusion.2
  8.7 0.0 all-gather.2.cloned.1.call-update
  8.7 121.7 %all-gather.2.cloned.1.call-done = bf16[768,1024]{1,0:T(8,128)(2,1)} async-done(((bf16[16,1024]{1,0:T(8,128)(2,1)}), bf16[768,1024]{1,0:T(8,128)(2,1)}) %all-gather.2.cloned.1.call-update) | async-done | bytes 1572880 | tf_op jit(solution)/shard_map/all_gather | solution.py:79
  130.4 0.0 copy-done
  130.4 3.2 fusion.3
  133.7 0.0 copy-start.2
  133.7 0.0 copy-start.3
  133.7 4.1 %all-to-all-start = ((f32[8,48,768]{2,1,0:T(8,128)}), f32[8,48,768]{2,1,0:T(8,128)S(1)}, u32[]{:S(2)}, u32[]{:S(2)}) async-start(f32[8,48,768]{2,1,0:T(8,128)} %bitcast.2), calls=%async_computation | async-start | bytes 2359296 | tf_op jit(solution)/shard_map/all_to_all | solution.py:23
  137.8 0.0 reduce-scatter.3.cloned.1.call-start
  137.8 0.0 copy-done.2
  137.9 0.0 copy-done.3
  137.9 11.0 %all-to-all-done = f32[8,48,768]{2,1,0:T(8,128)S(1)} async-done(((f32[8,48,768]{2,1,0:T(8,128)}), f32[8,48,768]{2,1,0:T(8,128)S(1)}, u32[]{:S(2)}, u32[]{:S(2)}) %all-to-all-start) | async-done | bytes 1179680 | tf_op jit(solution)/shard_map/all_to_all | solution.py:23
  148.9 0.1 reduce_sum.27
  149.0 0.1 fusion.1
  149.0 10.1 %psum.28 = f32[768]{0:T(1024)S(1)} all-reduce(f32[768]{0:T(1024)S(1)} %fusion.1), channel_id=1, replica_groups=mesh['head'=2,'seq_0'=4,'seq_1'=12,'mp_0'=4,'mp_1'=2] {'seq_0'}, use_global_device_ids=true, to_apply=%region_2.0 | all-reduce | flops 768 | bytes 6144 | tf_op jit(solution)/shard_map/psum | solution.py:29
  159.2 17.4 %psum.29 = f32[768]{0:T(1024)S(1)} all-reduce(f32[768]{0:T(1024)S(1)} %psum.28), channel_id=1, replica_groups=mesh['head'=2,'seq_0'=4,'seq_1'=12,'mp_0'=4,'mp_1'=2] {'seq_1'}, use_global_device_ids=true, to_apply=%region_3.0 | all-reduce | flops 768 | bytes 6144 | tf_op jit(solution)/shard_map/psum | solution.py:29
  176.6 7.8 %psum.30 = f32[768]{0:T(1024)S(1)} all-reduce(f32[768]{0:T(1024)S(1)} %psum.29), channel_id=1, replica_groups=mesh['head'=2,'seq_0'=4,'seq_1'=12,'mp_0'=4,'mp_1'=2] {'mp_0'}, use_global_device_ids=true, to_apply=%region_4.0 | all-reduce | flops 768 | bytes 6144 | tf_op jit(solution)/shard_map/psum | solution.py:29
  184.3 4.1 %psum.31 = f32[768]{0:T(1024)S(1)} all-reduce(f32[768]{0:T(1024)S(1)} %psum.30), channel_id=1, replica_groups=mesh['head'=2,'seq_0'=4,'seq_1'=12,'mp_0'=4,'mp_1'=2] {'mp_1'}, use_global_device_ids=true, to_apply=%region_5.0 | all-reduce | flops 768 | bytes 6144 | tf_op jit(solution)/shard_map/psum | solution.py:29
  188.4 0.1 multiply_convert_fusion
  188.6 10.4 %all_to_all.16 = bf16[8,48,768]{2,1,0:T(8,128)(2,1)S(1)} all-to-all(bf16[8,48,768]{2,1,0:T(8,128)(2,1)S(1)} %broadcast_in_dim.4), channel_id=1, replica_groups=mesh['head'=2,'seq_0'=4,'seq_1'=12,'mp_0'=4,'mp_1'=2] {'mp_0','mp_1'}, dimensions={0} | all-to-all | bytes 1179648 | tf_op jit(solution)/shard_map/all_to_all | solution.py:35
  199.0 0.3 copy.12
  199.3 1.0 convolution_bitcast_fusion
  200.3 1.9 copy.13
  202.1 0.0 copy-start.4
  202.1 0.0 reduce-scatter.3.cloned.1.call-update
  202.2 0.0 reduce-scatter.5.cloned.1.call-start
  202.2 69.1 %reduce-scatter.3.cloned.1.call-done = f32[4,16,1024]{2,1,0:T(8,128)} async-done(((f32[48,16,1024]{2,1,0:T(8,128)}), f32[4,16,1024]{2,1,0:T(8,128)}) %reduce-scatter.3.cloned.1.call-update) | async-done | bytes 262160 | tf_op jit(solution)/shard_map/reduce_scatter | solution.py:54
  271.3 0.0 reduce-scatter.5.cloned.1.call-update
  271.3 0.0 copy-done.4
  271.3 0.8 convolution_bitcast_fusion.1
  272.1 0.3 copy.18
  272.4 36.2 %reduce-scatter.5.cloned.1.call-done = f32[1,16,1024]{2,1,0:T(8,128)} async-done(((f32[4,16,1024]{2,1,0:T(8,128)}), f32[1,16,1024]{2,1,0:T(8,128)}) %reduce-scatter.5.cloned.1.call-update) | async-done | bytes 65552 | tf_op jit(solution)/shard_map/reduce_scatter | solution.py:54
  308.6 0.9 copy.17
  309.5 0.1 pad_maximum_fusion
  309.6 7.7 %broadcast_in_dim.10 = f32[2,1,409600]{2,1,0:T(1,128)S(1)} broadcast(f32[409600]{0:T(1024)S(1)} %pad_maximum_fusion), dimensions={2} | broadcast | bytes 4915200 | tf_op jit(solution)/shard_map/broadcast_in_dim | solution.py:34
  317.3 9.9 %all_to_all.17 = f32[2,1,409600]{2,1,0:T(1,128)} all-to-all(f32[2,1,409600]{2,1,0:T(1,128)S(1)} %broadcast_in_dim.10), channel_id=1, replica_groups=mesh['head'=2,'seq_0'=4,'seq_1'=12,'mp_0'=4,'mp_1'=2] {'head'}, dimensions={0} | all-to-all | bytes 6553600 | tf_op jit(solution)/shard_map/all_to_all | solution.py:35
  327.2 16.4 %reduce_sum.29 = f32[409600]{0:T(1024)S(1)} reduce(f32[2,1,409600]{2,1,0:T(1,128)} %all_to_all.17, f32[]{:T(128)} %constant.12.clone.1), dimensions={0,1}, to_apply=%region_8.0 | reduce | flops 409600 | bytes 4915204 | tf_op jit(solution)/shard_map/reduce_sum | solution.py:64
  343.6 1.3 slice.29
  344.9 0.0 copy-start.1
  344.9 2.6 slice.27
  347.4 0.6 convert_element_type.33
  348.1 0.0 copy-done.1
  348.1 0.6 convert_element_type.32
  (5 shorter events, 0.1 us)
Async XLA Ops:
  7.2 123.3 %copy-start = (bf16[384,1024]{1,0:T(8,128)(2,1)S(1)}, bf16[384,1024]{1,0:T(8,128)(2,1)}, u32[]{:S(2)}) copy-start(bf16[384,1024]{1,0:T(8,128)(2,1)} %param.7) | copy-start | bytes 2359300
  7.2 123.3 %all-gather.2.cloned.1.call-start = ((), (), s32[]{:S(2)}) async-start(), calls=%async_computation.5 | async-start | bytes 1605632 | tf_op jit(solution)/shard_map/all_gather | solution.py:79
  133.7 4.2 %copy-start.2 = (s32[1,768]{1,0:T(1,128)S(1)}, s32[1,768]{1,0:T(1,128)}, u32[]{:S(2)}) copy-start(s32[1,768]{1,0:T(1,128)} %param.8) | copy-start | bytes 9220
  133.7 4.2 %copy-start.3 = (f32[1,768]{1,0:T(1,128)S(1)}, f32[1,768]{1,0:T(1,128)}, u32[]{:S(2)}) copy-start(f32[1,768]{1,0:T(1,128)} %param.9) | copy-start | bytes 9220
  133.7 15.2 %all-to-all-start = ((f32[8,48,768]{2,1,0:T(8,128)}), f32[8,48,768]{2,1,0:T(8,128)S(1)}, u32[]{:S(2)}, u32[]{:S(2)}) async-start(f32[8,48,768]{2,1,0:T(8,128)} %bitcast.2), calls=%async_computation | async-start | bytes 2359296 | tf_op jit(solution)/shard_map/all_to_all | solution.py:23
  137.8 133.5 %reduce-scatter.3.cloned.1.call-start = ((), (), s32[]{:S(2)}) async-start(), calls=%async_computation.6 | async-start | bytes 3407872 | tf_op jit(solution)/shard_map/reduce_scatter | solution.py:54
  202.1 69.2 %copy-start.4 = (bf16[768,1024]{1,0:T(8,128)(2,1)S(1)}, bf16[768,1024]{1,0:T(8,128)(2,1)}, u32[]{:S(2)}) copy-start(bf16[768,1024]{1,0:T(8,128)(2,1)} %all-gather.2.cloned.1.call-done) | copy-start | bytes 4718596
  202.2 106.5 %reduce-scatter.5.cloned.1.call-start = ((), (), s32[]{:S(2)}) async-start(), calls=%async_computation.7 | async-start | bytes 327680 | tf_op jit(solution)/shard_map/reduce_scatter | solution.py:54
  344.9 3.2 copy-start.1
Sparse Core Ops, SparseCore 0:
  12.1 118.2 all-gather.1
  202.3 68.9 reduce-scatter.2
  274.4 34.1 reduce-scatter.4
where the time goes:
time: 356 us; the launch traced here: 355 us
  waiting for transfers between devices  238 us (67%)
  blocking collectives  59.7 us (17%)
  other arithmetic  18.8 us (5%)
  local copies, waits for them, and re-layouts  15.6 us (4%)
  between operations  13.9 us (4%)
  matrix products  4.99 us (1%)
  starting transfers between devices  4.22 us (1%)
    all_gather x1, waiting for transfers between devices, shards(): gathered = lax.all_gather(hidden, SEQ, axis=0, tiled=True)  122 us
    reduce_scatter x2, waiting for transfers between devices, own_block(): blocks = lax.psum_scatter(blocks, axes[k], scatter_dimension=0, tiled=True)  105 us
    psum x4, blocking collectives, one_axis_at_a_time(): value = lax.psum(value, axis)  39.4 us
    all_to_all x2, blocking collectives, sent_to_all(): return lax.all_to_all(copies, axis, split_axis=0, concat_axis=0, tiled=True)  20.3 us
    reduce_sum x1, other arithmetic, taken_together(): return sent_to_all(value, axis).sum(axis=0)  16.4 us
    all_to_all x1, waiting for transfers between devices, sum_at_owner(): lax.all_to_all(in_blocks(value, dim, devices), axis, 0, 0, tiled=True)  11 us
    broadcast_in_dim x2, local copies, waits for them, and re-layouts, sent_to_all(): copies = jnp.broadcast_to(value, (lax.axis_size(axis), *value.shape))  7.77 us
  transfers between devices with their start and end apart: 4, of which 4 were waited for; matrix products, arithmetic and copies ran while one was open for 0% of the time, Pallas kernels for 0%

commit v1 on v0

v1 whole, which is shorter than its diff:
```python
import functools

import jax
import jax.numpy as jnp
from jax import lax
from jax.experimental import pallas as pl
from jax.experimental.pallas import tpu as pltpu
from jax.sharding import Mesh
from jax.sharding import PartitionSpec as P

MESH = pl.DeviceIdType.MESH
SEQ = ("yh", "z")
MP = ("x", "yl")
F32, BF16 = jnp.float32, jnp.bfloat16

soft_cap = 30.0


def reach(n, j):
    far, near = n // 2, (n - 1) // 2
    return (far, near) if j % 2 == 0 else (near, far)


def step_kernel(
    sizes,
    trunk_ref,
    branch_ref,
    unembed_hbm,
    targets_ref,
    loss_grad_ref,
    d_branch_ref,
    d_trunk_ref,
    d_unembed_ref,
    unembed_ref,
    hid,
    part_out,
    part_in,
    tot_mp,
    tot_z,
    tot_y,
    tot_out,
    grads,
    grads_t,
    rows_part,
    rs_out,
    rs_in,
    y_out,
    y_in,
    own_rows,
    head_rows,
    own_weight,
    head_weight,
    local_sem,
    y_sems,
    ring_sems,
    part_sems,
    tot_mp_sems,
    tot_z_sems,
    tot_y_sems,
    grad_sems,
    rs_sems,
    yr_sems,
    head_sems,
):
    NH, NY, NZ, NX, NL = sizes
    NM = NX * NL
    head = lax.axis_index("head")
    yh, z = lax.axis_index("yh"), lax.axis_index("z")
    x, yl = lax.axis_index("x"), lax.axis_index("yl")
    block_rows = unembed_ref.shape[0]
    share = block_rows // NM
    rows = NY * NZ * hid.shape[1]
    RB, DS = hid.shape[1], hid.shape[2]

    def at_y(d):
        return lax.rem(yh + (d + NY), NY)

    def at_z(d):
        return lax.rem(z + (d + NZ), NZ)

    def mp_peer(d):
        dx, dl = d // NL, d % NL
        return lax.rem(x + dx, NX), lax.rem(yl + dl, NL)

    def mp_from(d):
        dx, dl = d // NL, d % NL
        return lax.rem(x + (NX - dx), NX), lax.rem(yl + (NL - dl), NL)

    def block(a, b):
        return a * NZ + b

    sent = []

    def copy(src, dst, sems, at, device):
        return pltpu.make_async_remote_copy(
            src_ref=src,
            dst_ref=dst,
            send_sem=sems.at[(0, *at)],
            recv_sem=sems.at[(1, *at)],
            device_id=device,
            device_id_type=MESH,
        )

    def send(*args):
        c = copy(*args)
        c.start()
        sent.append(c)

    load_unembed = pltpu.make_async_copy(unembed_hbm, unembed_ref, local_sem)
    load_unembed.start()

    barrier = pltpu.get_barrier_semaphore()
    peers = [{"yh": at_y(d)} for d in range(1, NY)]
    peers += [{"z": at_z(1)}, {"z": at_z(-1)}]
    for d in range(1, NM):
        px, pyl = mp_peer(d)
        peers.append({"x": px, "yl": pyl})
    peers.append({"head": 1 - head})
    for device in peers:
        pl.semaphore_signal(barrier, inc=1, device_id=device, device_id_type=MESH)

    me = block(yh, z)
    hid[me] = (trunk_ref[...].astype(F32) + branch_ref[0].astype(F32)).astype(BF16)
    pl.semaphore_wait(barrier, len(peers))

    ring = ({"z": at_z(1)}, {"z": at_z(-1)})

    def ring_send(way, k, j):
        origin = block(at_y(-j), at_z(-k if way == 0 else k))
        send(hid.at[origin], hid.at[origin], ring_sems, (way, k, j), ring[way])

    def ring_wait(way, k, j):
        origin = block(at_y(-j), at_z(-k if way == 0 else k))
        copy(hid.at[origin], hid.at[origin], ring_sems, (way, k - 1, j), ring[way]).wait_recv()

    for d in range(1, NY):
        send(hid.at[me], hid.at[me], y_sems, (d,), {"yh": at_y(d)})
    order = [j for j in (0, 1, 3, 2) if j < NY]
    for j in order:
        if j:
            origin = block(at_y(-j), z)
            copy(hid.at[origin], hid.at[origin], y_sems, (j,), {"yh": at_y(j)}).wait_recv()
        for way in (0, 1):
            if reach(NZ, j)[way] > 0:
                ring_send(way, 0, j)
    for k in range(1, NZ // 2 + 1):
        for j in order:
            for way in (0, 1):
                limit = reach(NZ, j)[way]
                if k <= limit:
                    ring_wait(way, k, j)
                    if k < limit:
                        ring_send(way, k, j)

    load_unembed.wait()
    lanes = min(256, rows)
    for c in range(rows // lanes):
        chunk = hid[c * (lanes // RB) : (c + 1) * (lanes // RB)].reshape(lanes, DS)
        partial = lax.dot_general(
            unembed_ref[...], chunk, (((1,), (1,)), ((), ())), preferred_element_type=F32
        )
        part_out[:, :, c * lanes : (c + 1) * lanes] = partial.astype(BF16).reshape(NM, share, lanes)
    mine = x * NL + yl
    for d in range(1, NM):
        px, pyl = mp_peer(d)
        send(part_out.at[px * NL + pyl], part_in.at[d], part_sems, (d,), {"x": px, "yl": pyl})
    scores = part_out[mine].astype(F32)
    for d in range(1, NM):
        px, pyl = mp_peer(d)
        copy(part_in.at[d], part_in.at[d], part_sems, (d,), {"x": px, "yl": pyl}).wait_recv()
        scores = scores + part_in[d].astype(F32)
    squashed = jnp.tanh(scores / soft_cap)
    exponent = jnp.exp(soft_cap * squashed)

    total = jnp.sum(exponent, axis=0, keepdims=True)
    tot_out[0] = total
    for d in range(1, NM):
        px, pyl = mp_peer(d)
        send(tot_out.at[0], tot_mp.at[d], tot_mp_sems, (d,), {"x": px, "yl": pyl})
    for d in range(1, NM):
        px, pyl = mp_peer(d)
        copy(tot_mp.at[d], tot_mp.at[d], tot_mp_sems, (d,), {"x": px, "yl": pyl}).wait_recv()
        total = total + tot_mp[d]
    tot_out[1] = total
    for d in range(1, NZ):
        send(tot_out.at[1], tot_z.at[d], tot_z_sems, (d,), {"z": at_z(d)})
    for d in range(1, NZ):
        copy(tot_z.at[d], tot_z.at[d], tot_z_sems, (d,), {"z": at_z(d)}).wait_recv()
        total = total + tot_z[d]
    tot_out[2] = total
    for d in range(1, NY):
        send(tot_out.at[2], tot_y.at[d], tot_y_sems, (d,), {"yh": at_y(d)})
    for d in range(1, NY):
        copy(tot_y.at[d], tot_y.at[d], tot_y_sems, (d,), {"yh": at_y(d)}).wait_recv()
        total = total + tot_y[d]

    first_vocab = me * block_rows + mine * share
    vocab_ids = first_vocab + lax.broadcasted_iota(jnp.int32, (share, rows), 0)
    onehot = (vocab_ids == targets_ref[...]).astype(F32)
    slope = loss_grad_ref[...] * (exponent / total - onehot) * (1.0 - squashed * squashed)
    grads[mine] = slope.astype(BF16)
    for d in range(1, NM):
        px, pyl = mp_peer(d)
        send(grads.at[mine], grads.at[mine], grad_sems, (d,), {"x": px, "yl": pyl})
    for d in range(1, NM):
        px, pyl = mp_from(d)
        origin = px * NL + pyl
        copy(grads.at[origin], grads.at[origin], grad_sems, (d,), {"x": px, "yl": pyl}).wait_recv()

    for c in range(rows // 128):
        piece = grads[:, :, c * 128 : (c + 1) * 128].reshape(block_rows, 128)
        grads_t[c * 128 : (c + 1) * 128, :] = piece.T
    for c in range(rows // lanes):
        partial = jnp.dot(
            grads_t[c * lanes : (c + 1) * lanes, :], unembed_ref[...], preferred_element_type=F32
        )
        rows_part[c * (lanes // RB) : (c + 1) * (lanes // RB)] = partial.reshape(lanes // RB, RB, DS)

    back = [j for j in (2, 1, 3, 0) if j < NY]

    def rs_step(way, i, j):
        limit = reach(NZ, j)[way]
        ahead = limit - i
        target = block(at_y(j), at_z(ahead if way == 0 else -ahead))
        value = rows_part[target]
        if i > 0:
            copy(
                rs_in.at[way, i - 1, j], rs_in.at[way, i - 1, j], rs_sems, (way, i - 1, j), ring[way]
            ).wait_recv()
            value = value + rs_in[way, i - 1, j].astype(F32)
        if i < limit:
            rs_out[way, i, j] = value.astype(BF16)
            send(rs_out.at[way, i, j], rs_in.at[way, i, j], rs_sems, (way, i, j), ring[way])

    for j in back:
        for way in (0, 1):
            if reach(NZ, j)[way] > 0:
                rs_step(way, 0, j)

    all_grads = grads[...].reshape(block_rows, rows)
    cols = min(256, DS)
    for c in range(DS // cols):
        own_weight[:, c * cols : (c + 1) * cols] = jnp.dot(
            all_grads,
            hid[:, :, c * cols : (c + 1) * cols].reshape(rows, cols),
            preferred_element_type=F32,
        )
    send(own_weight, head_weight, head_sems, (0,), {"head": 1 - head})

    for i in range(1, NZ // 2 + 1):
        for j in back:
            for way in (0, 1):
                if i < reach(NZ, j)[way]:
                    rs_step(way, i, j)
    for j in back:
        value = rows_part[block(at_y(j), z)]
        for way in (0, 1):
            limit = reach(NZ, j)[way]
            if limit > 0:
                slot = rs_in.at[way, limit - 1, j]
                copy(slot, slot, rs_sems, (way, limit - 1, j), ring[way]).wait_recv()
                value = value + rs_in[way, limit - 1, j].astype(F32)
        if j:
            y_out[j] = value.astype(BF16)
            send(y_out.at[j], y_in.at[j], yr_sems, (j,), {"yh": at_y(j)})
        else:
            row_grad = value
    copy(own_weight, head_weight, head_sems, (0,), {"head": 1 - head}).wait_recv()
    d_unembed_ref[...] = own_weight[...] + head_weight[...]
    for j in range(1, NY):
        copy(y_in.at[j], y_in.at[j], yr_sems, (j,), {"yh": at_y(j)}).wait_recv()
        row_grad = row_grad + y_in[j].astype(F32)
    own_rows[...] = row_grad
    send(own_rows, head_rows, head_sems, (1,), {"head": 1 - head})
    d_branch_ref[0] = row_grad.astype(BF16)
    copy(own_rows, head_rows, head_sems, (1,), {"head": 1 - head}).wait_recv()
    d_trunk_ref[...] = (row_grad + head_rows[...]).astype(BF16)
    for c in sent:
        c.wait_send()


def shards(sizes, trunk, branch, unembed, targets, loss_grad):
    NH, NY, NZ, NX, NL = sizes
    NM = NX * NL
    RB, DS = trunk.shape
    VB = unembed.shape[0]
    share, rows = VB // NM, NY * NZ * RB
    steps = NZ // 2
    sem = pltpu.SemaphoreType.DMA
    vmem = pl.BlockSpec(memory_space=pltpu.VMEM)
    return pl.pallas_call(
        functools.partial(step_kernel, sizes),
        out_shape=(
            jax.ShapeDtypeStruct((1, RB, DS), BF16),
            jax.ShapeDtypeStruct((RB, DS), BF16),
            jax.ShapeDtypeStruct((VB, DS), F32),
        ),
        in_specs=[vmem, vmem, pl.BlockSpec(memory_space=pl.ANY), vmem, vmem],
        out_specs=(vmem, vmem, vmem),
        scratch_shapes=[
            pltpu.VMEM((VB, DS), BF16),
            pltpu.VMEM((NY * NZ, RB, DS), BF16),
            pltpu.VMEM((NM, share, rows), BF16),
            pltpu.VMEM((NM, share, rows), BF16),
            pltpu.VMEM((NM, 1, rows), F32),
            pltpu.VMEM((NZ, 1, rows), F32),
            pltpu.VMEM((NY, 1, rows), F32),
            pltpu.VMEM((3, 1, rows), F32),
            pltpu.VMEM((NM, share, rows), BF16),
            pltpu.VMEM((rows, VB), BF16),
            pltpu.VMEM((NY * NZ, RB, DS), F32),
            pltpu.VMEM((2, steps, NY, RB, DS), BF16),
            pltpu.VMEM((2, steps, NY, RB, DS), BF16),
            pltpu.VMEM((NY, RB, DS), BF16),
            pltpu.VMEM((NY, RB, DS), BF16),
            pltpu.VMEM((RB, DS), F32),
            pltpu.VMEM((RB, DS), F32),
            pltpu.VMEM((VB, DS), F32),
            pltpu.VMEM((VB, DS), F32),
            sem,
            sem((2, NY)),
            sem((2, 2, steps, NY)),
            sem((2, NM)),
            sem((2, NM)),
            sem((2, NZ)),
            sem((2, NY)),
            sem((2, NM)),
            sem((2, 2, steps, NY)),
            sem((2, NY)),
            sem((2, 2)),
        ],
        compiler_params=pltpu.CompilerParams(
            collective_id=0, has_side_effects=True, vmem_limit_bytes=48 * 1024 * 1024
        ),
    )(trunk, branch, unembed, targets, loss_grad)


def solution(mesh, sizes=(2, 4, 12, 4, 2)):
    split = Mesh(mesh.devices.reshape(sizes), ("head", "yh", "z", "x", "yl"))
    return jax.shard_map(
        functools.partial(shards, sizes),
        mesh=split,
        in_specs=(P(SEQ, MP), P("head", SEQ, MP), P(SEQ, MP), P("head", None), P("head", None)),
        out_specs=(P("head", SEQ, MP), P(SEQ, MP), P(SEQ, MP)),
        check_vma=False,
    )
```

time: 356 us -> 110 us (0.31)
  waiting for transfers between devices: 238 us -> 0 us
  Pallas kernels: 0 us -> 103 us
  blocking collectives: 59.7 us -> 0 us
  other arithmetic: 18.8 us -> 0 us
  between operations: 13.9 us -> 0.65 us
  local copies, waits for them, and re-layouts: 15.6 us -> 6.38 us
  matrix products: 4.99 us -> 0 us
  starting transfers between devices: 4.22 us -> 0 us
    all_gather x1 -> x0, waiting for transfers between devices: 122 us -> none  [shards(): gathered = lax.all_gather(hidden, SEQ, axis=0, tiled=True)]
    reduce_scatter x2 -> x0, waiting for transfers between devices: 105 us -> none  [own_block(): blocks = lax.psum_scatter(blocks, axes[k], scatter_dimension=0, tiled=True)]
    pallas_call x0 -> x1, Pallas kernels: none -> 103 us  [shards(): pl.pallas_call(functools.partial(step_kernel, sizes), out_shape=(jax.Shap...]
    psum x4 -> x0, blocking collectives: 39.4 us -> none  [one_axis_at_a_time(): value = lax.psum(value, axis)]
    all_to_all x2 -> x0, blocking collectives: 20.3 us -> none  [sent_to_all(): return lax.all_to_all(copies, axis, split_axis=0, concat_axis=0, tiled=True)]
    reduce_sum x3 -> x0, other arithmetic: 16.5 us -> none  [the longest x1 16.4 us: taken_together(): return sent_to_all(value, axis).sum(axis=0)]
    all_to_all x1 -> x0, waiting for transfers between devices: 11 us -> none  [sum_at_owner(): lax.all_to_all(in_blocks(value, dim, devices), axis, 0, 0, tiled=True)]
    broadcast_in_dim x2 -> x0, local copies, waits for them, and re-layouts: 7.77 us -> none  [sent_to_all(): copies = jnp.broadcast_to(value, (lax.axis_size(axis), *value.shape))]
  transfers between devices with their start and end apart: 4 -> 0, of which waited for: 4 -> 0; matrix products, arithmetic and copies ran while one was open for 0% -> 0% of each run, Pallas kernels for 0% -> 0%
where the time goes in v1:
time: 110 us
  Pallas kernels  103 us (94%)
  local copies, waits for them, and re-layouts  6.38 us (6%)
    pallas_call x1, Pallas kernels, shards(): pl.pallas_call(functools.partial(step_kernel, sizes), out_shape=(jax.Shap...  103 us
    unnamed x13, local copies, waits for them, and re-layouts  6.38 us

profile of v1, /device:TPU:1, one launch (start us, length us, event | category | flops | bytes accessed | tf_op | source)
XLA Modules:
  0.0 110.1 jit_solution(6439048018533759276)
XLA Ops:
  0.6 0.0 copy-start
  0.6 1.1 %copy-done = bf16[384,1024]{1,0:T(8,128)(2,1)S(1)} copy-done((bf16[384,1024]{1,0:T(8,128)(2,1)S(1)}, bf16[384,1024]{1,0:T(8,128)(2,1)}, u32[]{:S(2)}) %copy-start) | copy-done | bytes 786456
  1.8 0.0 copy-start.1
  1.8 0.8 copy-done.1
  2.5 0.0 copy-start.2
  2.5 0.8 copy-done.2
  3.3 0.0 copy-start.3
  3.3 0.7 copy-done.3
  4.0 0.0 copy-start.4
  4.0 0.7 copy-done.4
  4.7 103.1 %shard_map.76 = (bf16[1,16,1024]{2,1,0:T(8,128)(2,1)S(1)}, bf16[16,1024]{1,0:T(8,128)(2,1)S(1)}, f32[384,1024]{1,0:T(8,128)S(1)}) custom-call(bf16[16,1024]{1,0:T(8,128)(2,1)S(1)} %copy-done.1, bf16[1,16,1024]{2,1,0:T(8,128)(2,1)S(1)} %copy-done.2, bf16[384,1024]{1,0:T(8,128)(2,1)S(1)} %copy-done, s32[1,768]{1,0:T(1,128)S(1)} %copy-done.3, ...), custom_call_target="tpu_custom_call" | custom-call | tf_op jit(solution)/shard_map/pallas_call | solution.py:291
  107.7 0.6 copy.11
  108.4 0.6 copy.12
  109.0 1.1 %copy.13 = f32[384,1024]{1,0:T(8,128)} copy(f32[384,1024]{1,0:T(8,128)S(1)} %get-tuple-element.8) | data formatting | bytes 3145728
Async XLA Ops:
  0.6 1.1 %copy-start = (bf16[384,1024]{1,0:T(8,128)(2,1)S(1)}, bf16[384,1024]{1,0:T(8,128)(2,1)}, u32[]{:S(2)}) copy-start(bf16[384,1024]{1,0:T(8,128)(2,1)} %unembed_hbm.1) | copy-start | bytes 2359300
  1.8 0.8 copy-start.1
  2.5 0.8 copy-start.2
  3.3 0.7 copy-start.3
  4.0 0.7 copy-start.4
